TPU v7x, 128 devices: a whole 4x4x4 slice. The times are simulated.
128 devices in a mesh: dp: 8 (over z, core), cp: 16 (over x, y).
Axes of the slice: x: 4, y: 4, z: 4, core: 2. Of those that a mesh axis runs over, the one named last changes fastest.
Arguments:
- row_owner: int32 [16384, 1], P(('dp', 'cp')), may hold values from 0 to 127; in each aligned block of 128 rows (0 to 127, 128 to 255, ...) at most 4 rows name the same one
- slot_row: int32 [16384], P(('dp', 'cp')), may hold values from 0 to 2559
- hot_table: bfloat16 [65536, 512], P(('dp', 'cp')), may hold values from -6 to 6
- cold_table: bfloat16 [262144, 128], P(('dp', 'cp')), may hold values from -6 to 6
- cold_projection: bfloat16 [128, 512], replicated, may hold values from -0.5 to 0.5
- joined_weight: bfloat16 [512, 2048], replicated, may hold values from -0.25 to 0.25
- output_weight: bfloat16 [512, 512], replicated, may hold values from -0.25 to 0.25
- cotangent: bfloat16 [16384, 512], P(('dp', 'cp')), may hold values from -6 to 6
Outputs:
- layer_out: bfloat16 [16384, 512], P(('dp', 'cp'))
- hot_gradient: float32 [65536, 512], P(('dp', 'cp'))
- cold_gradient: float32 [262144, 128], P(('dp', 'cp'))
- projection_gradient: float32 [128, 512], replicated
- joined_gradient: float32 [512, 2048], replicated
- output_gradient: float32 [512, 512], replicated
Inputs may be any that keep to these rules, and one draw needn't show every extreme that they name: `row_owner`: in each aligned block of 128 rows (the rows of one device) no owner is named by more than 4 rows.
All inputs are finite; a program needn't handle non-finite values.
Results may differ from a plain program's by a relative error of at most 0.013.
Values may be sent and summed in bfloat16 or wider, within the bound.
A program may use at most 128 MiB of HBM per device.

v0:
```python
import math
import jax
import jax.numpy as jnp
from jax import lax
from jax.sharding import PartitionSpec as P

HEADS = 8
EPSILON = 1e-05
block_limit = 1024


def side_by_side(arrays, axis, dim, along):
    ends, at = ([], 0)
    for a in arrays[:-1]:
        at += a.shape[along]
        ends.append(at)
    both = jnp.concatenate(arrays, axis=along)
    return tuple(jnp.split(lax.all_gather(both, axis, axis=dim, tiled=True), ends, axis=along))


def cut_along(x, dim, length):
    dims = x.shape
    blocks = x.reshape(*dims[:dim], length, dims[dim] // length, *dims[dim + 1 :])
    return jnp.moveaxis(blocks, dim, 0)


def edges_of(length, count):
    unit = 8 if length >= 8 * count else 1
    return [length // unit * k // count * unit for k in range(1, count)]


def in_order(blocks, dim):
    blocks = jnp.moveaxis(blocks, 0, dim)
    dims = blocks.shape
    return blocks.reshape(*dims[:dim], dims[dim] * dims[dim + 1], *dims[dim + 2 :])


def several_exchanges(x, axis, pieces, split_dim, concat_dim):
    blocks = cut_along(x, split_dim, lax.axis_size(axis))
    split_at = max(range(1, max(2, blocks.ndim - 1)), key=lambda d: blocks.shape[d])
    gathered = []
    for piece in jnp.split(blocks, edges_of(blocks.shape[split_at], pieces), axis=split_at):
        if piece.size:
            gathered.append(lax.all_to_all(piece, axis, split_axis=0, concat_axis=0, tiled=True))
    return in_order(jnp.concatenate(gathered, axis=split_at), concat_dim)


def silu_slope(values):
    sigmoid_v = jax.nn.sigmoid(values)
    return sigmoid_v * (1.0 + values * (1.0 - sigmoid_v))


def layer_normalize(values):
    average = jnp.mean(values, axis=-1, keepdims=True)
    centred = values - average
    inverse = lax.rsqrt(jnp.mean(centred * centred, axis=-1, keepdims=True) + EPSILON)
    return (centred * inverse, inverse)


def normalize_back(gradient, normed, inverse):
    first_term = jnp.mean(gradient, axis=-1, keepdims=True)
    second_term = jnp.mean(gradient * normed, axis=-1, keepdims=True)
    return (gradient - first_term - normed * second_term) * inverse


def masked_scores(query_heads, key_heads, query_index, key_index, score_scale):
    scores = (
        jnp.einsum("qhd,khd->hqk", query_heads, key_heads, preferred_element_type=jnp.float32)
        * score_scale
    )
    allowed = (key_index[None, :] <= query_index[:, None])[None]
    weights = jnp.where(allowed, jax.nn.silu(scores), 0.0).astype(jnp.bfloat16)
    return (scores, allowed, weights)


def score_deltas(
    query_heads, key_heads, value_heads, delta_heads, query_index, key_index, score_scale
):
    scores, allowed, weights = masked_scores(
        query_heads, key_heads, query_index, key_index, score_scale
    )
    delta_weights = jnp.einsum(
        "qhd,khd->hqk", delta_heads, value_heads, preferred_element_type=jnp.float32
    )
    delta_scores = jnp.where(allowed, delta_weights * silu_slope(scores) * score_scale, 0.0).astype(
        jnp.bfloat16
    )
    return (weights, delta_scores)


def local(
    row_owner,
    slot_row,
    hot_table,
    cold_table,
    cold_projection,
    joined_weight,
    output_weight,
    cotangent,
):
    tokens_here = slot_row.shape[0]
    model_width = output_weight.shape[0]
    hot_count = hot_table.shape[0]
    cold_count = cold_table.shape[0]
    cold_width = cold_table.shape[1]
    head_count = HEADS
    head_size = model_width // head_count
    score_scale = 1.0 / math.sqrt(head_size)
    devices = lax.axis_size(("dp", "cp"))
    group_index = lax.axis_index("cp")
    capacity = 2 * tokens_here // devices + 2
    owners = row_owner[:, 0]
    is_hot = slot_row < hot_count
    is_cold = jnp.logical_not(is_hot)
    onehot = (owners[:, None] == jnp.arange(devices, dtype=jnp.int32)[None, :]).astype(jnp.bfloat16)
    lower_mask = (jnp.arange(tokens_here)[:, None] > jnp.arange(tokens_here)[None, :]).astype(
        jnp.bfloat16
    )
    earlier = jnp.dot(lower_mask, onehot, preferred_element_type=jnp.float32)
    rank_in_owner = jnp.sum(earlier * onehot.astype(jnp.float32), axis=1).astype(jnp.int32)
    slot_index = owners * capacity + rank_in_owner
    requests = (
        jnp.full((devices * capacity,), -1, jnp.int32)
        .at[slot_index]
        .set(slot_row)
        .reshape(devices, capacity)
    )
    asked_rows = lax.all_to_all(requests, ("dp", "cp"), split_axis=0, concat_axis=0, tiled=True)
    valid_hot = (asked_rows >= 0) & (asked_rows < hot_count)
    valid_cold = asked_rows >= hot_count
    nothing = jnp.zeros((), jnp.bfloat16)
    hot_pick = jnp.where(
        valid_hot[..., None], hot_table[jnp.clip(asked_rows, 0, hot_count - 1)], nothing
    )
    cold_pick = jnp.where(
        valid_cold[..., None],
        cold_table[jnp.clip(asked_rows - hot_count, 0, cold_count - 1)],
        nothing,
    )
    padded = jnp.pad(cold_pick, ((0, 0), (0, 0), (0, model_width - cold_width)))
    packed = jnp.where(valid_hot[..., None], hot_pick, padded)
    returned = lax.all_to_all(packed, ("dp", "cp"), split_axis=0, concat_axis=0, tiled=True)
    fetched = returned.reshape(devices * capacity, model_width)[slot_index]
    cold_vector = fetched[:, :cold_width]
    cold_embed = jnp.dot(cold_vector, cold_projection, preferred_element_type=jnp.float32)
    embedded = jnp.where(is_hot[:, None], fetched.astype(jnp.float32), cold_embed)
    normed, inverse = layer_normalize(embedded)
    normed_low = normed.astype(jnp.bfloat16)
    hidden = jnp.dot(normed_low, joined_weight, preferred_element_type=jnp.float32)
    active = jax.nn.silu(hidden).astype(jnp.bfloat16)
    gate_part = active[:, :model_width]
    attention_rows = active[:, model_width:]
    segments = [(0, tokens_here, group_index * tokens_here)]
    value_rows = attention_rows[:, :model_width]
    query_rows = attention_rows[:, model_width : 2 * model_width]
    key_rows = attention_rows[:, 2 * model_width :]
    local_index = jnp.concatenate(
        [first + jnp.arange(count, dtype=jnp.int32) for start, count, first in segments]
    )
    all_keys, all_values = side_by_side((key_rows, value_rows), "cp", 0, 1)
    length = all_keys.shape[0]
    key_span = min(length, block_limit)
    heads_shape = (tokens_here, head_count, head_size)
    query_heads = query_rows.reshape(heads_shape)

    def key_slices(counter):
        offset = counter * key_span
        key_block = lax.dynamic_slice_in_dim(all_keys, offset, key_span, 0).reshape(
            key_span, head_count, head_size
        )
        value_block = lax.dynamic_slice_in_dim(all_values, offset, key_span, 0).reshape(
            key_span, head_count, head_size
        )
        key_index = offset + jnp.arange(key_span, dtype=jnp.int32)
        return (offset, key_block, value_block, key_index)

    def blocks_needed(first, count):
        return (first + count + key_span - 1) // key_span

    start, count, first = segments[0]
    segment_queries = query_heads
    segment_index = first + jnp.arange(count, dtype=jnp.int32)

    def forward_step(
        counter, running, segment_queries=segment_queries, segment_index=segment_index
    ):
        offset, key_block, value_block, key_index = key_slices(counter)
        scores, allowed, weights = masked_scores(
            segment_queries, key_block, segment_index, key_index, score_scale
        )
        return running + jnp.einsum(
            "hqk,khd->qhd", weights, value_block, preferred_element_type=jnp.float32
        )

    empty_part = jnp.zeros((count, head_count, head_size), jnp.float32)
    attended_parts = lax.fori_loop(0, blocks_needed(first, count), forward_step, empty_part)
    attended = attended_parts.reshape(tokens_here, model_width)
    mixed, inverse_mix = layer_normalize(attended)
    gated = (mixed * gate_part.astype(jnp.float32)).astype(jnp.bfloat16)
    branch = jnp.dot(gated, output_weight, preferred_element_type=jnp.float32)
    layer_out = (embedded + branch).astype(jnp.bfloat16)
    delta_gated = jnp.dot(cotangent, output_weight.T, preferred_element_type=jnp.float32)
    delta_gate = delta_gated * mixed
    delta_attended = normalize_back(
        delta_gated * gate_part.astype(jnp.float32), mixed, inverse_mix
    ).astype(jnp.bfloat16)
    delta_heads = delta_attended.reshape(heads_shape)
    empty_heads = jnp.zeros(heads_shape, jnp.float32)
    start, count, first = segments[0]
    segment_queries = query_heads
    segment_deltas = delta_heads
    segment_index = first + jnp.arange(count, dtype=jnp.int32)

    def query_step(
        counter,
        running,
        segment_queries=segment_queries,
        segment_deltas=segment_deltas,
        segment_index=segment_index,
    ):
        offset, key_block, value_block, key_index = key_slices(counter)
        weights, delta_scores = score_deltas(
            segment_queries,
            key_block,
            value_block,
            segment_deltas,
            segment_index,
            key_index,
            score_scale,
        )
        return running + jnp.einsum(
            "hqk,khd->qhd", delta_scores, key_block, preferred_element_type=jnp.float32
        )

    empty_part = jnp.zeros((count, head_count, head_size), jnp.float32)
    query_parts = lax.fori_loop(0, blocks_needed(first, count), query_step, empty_part)
    key_heads = key_rows.reshape(heads_shape)
    value_heads = value_rows.reshape(heads_shape)
    key_lowest = jnp.min(local_index)
    query_piece, delta_piece = side_by_side((query_rows, delta_attended), "cp", 0, 1)
    row_count = query_piece.shape[0]
    sub_rows = math.gcd(row_count, block_limit)

    def inner_step(counter, partial_sums):
        start_row = counter * sub_rows
        query_block = lax.dynamic_slice_in_dim(query_piece, start_row, sub_rows, 0).reshape(
            sub_rows, head_count, head_size
        )
        delta_block = lax.dynamic_slice_in_dim(delta_piece, start_row, sub_rows, 0).reshape(
            sub_rows, head_count, head_size
        )
        query_index = start_row + jnp.arange(sub_rows, dtype=jnp.int32)

        def accumulate(sums_in):
            weights, delta_scores = score_deltas(
                query_block,
                key_heads,
                value_heads,
                delta_block,
                query_index,
                local_index,
                score_scale,
            )
            key_sum = sums_in[0] + jnp.einsum(
                "hqk,qhd->khd", delta_scores, query_block, preferred_element_type=jnp.float32
            )
            value_sum = sums_in[1] + jnp.einsum(
                "hqk,qhd->khd", weights, delta_block, preferred_element_type=jnp.float32
            )
            return (key_sum, value_sum)

        return lax.cond(
            jnp.max(query_index) >= key_lowest, accumulate, lambda sums_in: sums_in, partial_sums
        )

    key_sum, value_sum = lax.fori_loop(
        0, row_count // sub_rows, inner_step, (empty_heads, empty_heads)
    )
    delta_key = key_sum.reshape(tokens_here, model_width)
    delta_value = value_sum.reshape(tokens_here, model_width)
    attention_grads = jnp.concatenate(
        [delta_value, query_parts.reshape(tokens_here, model_width), delta_key], axis=1
    )
    delta_active = jnp.concatenate([delta_gate, attention_grads], axis=1)
    delta_hidden = (delta_active * silu_slope(hidden)).astype(jnp.bfloat16)
    delta_normed = jnp.dot(delta_hidden, joined_weight.T, preferred_element_type=jnp.float32)
    delta_embed = normalize_back(delta_normed, normed, inverse) + cotangent.astype(jnp.float32)
    cold_float = jnp.where(is_cold[:, None], cold_vector.astype(jnp.float32), 0.0)
    joined_local = jnp.dot(normed_low.T, delta_hidden, preferred_element_type=jnp.float32)
    output_local = jnp.dot(gated.T, cotangent, preferred_element_type=jnp.float32)
    projection_local = jnp.dot(cold_float.T, delta_embed, precision=lax.Precision.HIGHEST)
    joined_sum, output_sum, projection_sum = (
        lax.psum(joined_local.astype(jnp.bfloat16), ("dp", "cp")).astype(jnp.float32),
        lax.psum(output_local.astype(jnp.bfloat16), ("dp", "cp")).astype(jnp.float32),
        lax.psum(projection_local.astype(jnp.bfloat16), ("dp", "cp")).astype(jnp.float32),
    )
    norm_scale = (tokens_here * devices) ** (-0.5)
    cold_event = jnp.where(
        is_cold[:, None],
        jnp.dot(
            delta_embed, cold_projection.astype(jnp.float32).T, precision=lax.Precision.HIGHEST
        ),
        0.0,
    )
    hot_event = jnp.where(is_hot[:, None], delta_embed, 0.0)
    padded_event = jnp.pad(cold_event, ((0, 0), (0, model_width - cold_width)))
    packed_event = jnp.where(is_hot[:, None], hot_event, padded_event)
    buffer = (
        jnp.zeros((devices * capacity, model_width), jnp.float32)
        .at[slot_index]
        .set(packed_event)
        .reshape(devices, capacity, model_width)
    )
    arrived = several_exchanges(buffer.astype(jnp.bfloat16), ("dp", "cp"), 2, 0, 0).astype(
        buffer.dtype
    )
    cold_arrived = arrived[..., :cold_width]
    hot_target = jnp.where(valid_hot, asked_rows, hot_count).reshape(-1)
    cold_target = jnp.where(valid_cold, asked_rows - hot_count, cold_count).reshape(-1)
    hot_gradient = (
        jnp.zeros((hot_count, model_width), jnp.float32)
        .at[hot_target]
        .add(arrived.reshape(-1, model_width), mode="drop")
    )
    cold_gradient = (
        jnp.zeros((cold_count, cold_width), jnp.float32)
        .at[cold_target]
        .add(cold_arrived.reshape(-1, cold_width), mode="drop")
    )
    return (
        layer_out,
        hot_gradient,
        cold_gradient,
        projection_sum * norm_scale,
        joined_sum * norm_scale,
        output_sum * norm_scale,
    )


def solution(mesh):
    placed = (
        P(("dp", "cp"), None),
        P(("dp", "cp")),
        P(("dp", "cp"), None),
        P(("dp", "cp"), None),
        P(),
        P(),
        P(),
        P(("dp", "cp"), None),
    )
    return jax.shard_map(
        local,
        mesh=mesh,
        in_specs=placed,
        out_specs=(
            P(("dp", "cp"), None),
            P(("dp", "cp"), None),
            P(("dp", "cp"), None),
            P(),
            P(),
            P(),
        ),
        check_vma=False,
    )
```

profile of v0, /device:TPU:1, one launch (start us, length us, event | category | flops | bytes accessed | tf_op | source)
XLA Modules:
  0.0 425.6 jit_solution(10073714078295284084)
XLA Ops:
  7.2 1.0 fusion.46
  8.9 1.1 scatter_custom_fusion
  10.1 20.9 %all_to_all.27 = s32[128,1,4]{2,1,0:T(1,128)S(1)} all-to-all(s32[128,1,4]{2,1,0:T(1,128)S(1)} %bitcast.196), channel_id=1, replica_groups=mesh['dp'=8,'cp'=16] {'dp','cp'}, dimensions={0} | all-to-all | bytes 4096 | tf_op jit(solution)/shard_map/all_to_all | solution.py:128
  31.7 3.1 gather_fusion
  35.9 1.3 gather_fusion.1
  37.5 2.2 pad_select_fusion
  39.7 4.5 %all-to-all-start.1 = ((bf16[128,4,512]{2,1,0:T(4,128)(2,1)}), bf16[128,4,512]{2,1,0:T(4,128)(2,1)S(1)}, u32[]{:S(2)}, u32[]{:S(2)}) async-start(bf16[128,4,512]{2,1,0:T(4,128)(2,1)} %pad_select_fusion), calls=%async_computation.1 | async-start | bytes 1048576 | tf_op jit(solution)/shard_map/all_to_all | solution.py:142
  44.9 12.7 %all-to-all-done.1 = bf16[128,4,512]{2,1,0:T(4,128)(2,1)S(1)} async-done(((bf16[128,4,512]{2,1,0:T(4,128)(2,1)}), bf16[128,4,512]{2,1,0:T(4,128)(2,1)S(1)}, u32[]{:S(2)}, u32[]{:S(2)}) %all-to-all-start.1) | async-done | bytes 524320 | tf_op jit(solution)/shard_map/all_to_all | solution.py:142
  59.5 1.5 multiply_convert_fusion
  63.7 45.9 %all-gather.3.cloned.1.call-done = bf16[2048,1024]{1,0:T(8,128)(2,1)} async-done(((bf16[128,1024]{1,0:T(8,128)(2,1)}), bf16[2048,1024]{1,0:T(8,128)(2,1)}) %all-gather.3.cloned.1.call-update) | async-done | bytes 4194320 | tf_op jit(solution)/shard_map/all_gather | solution.py:18
  109.6 4.5 %fusion.84 = (bf16[2048,512]{1,0:T(8,128)(2,1)}, bf16[2048,512]{1,0:T(8,128)(2,1)}) fusion(bf16[2048,1024]{1,0:T(8,128)(2,1)} %all-gather.3.cloned.1.call-done), kind=kLoop, calls=%fused_computation.161 | loop fusion | bytes 8388608 | tf_op jit(solution)/shard_map/split | solution.py:18
  114.2 4.0 copy.83
  118.1 4.0 copy.84
  122.8 6.8 %while.38 = (s32[]{:T(128)}, f32[128,8,64]{0,2,1:T(8,128)}, s32[]{:T(128)}, bf16[2048,512]{0,1:T(8,128)(2,1)}, bf16[2048,512]{0,1:T(8,128)(2,1)}, /*index=5*/bf1...) while((s32[]{:T(128)}, f32[128,8,64]{0,2,1:T(8,128)}, ...), condition=%wide.region_5.6_spmd.clone, body=%wide.region_4.5_spmd.clone.sunk | while | flops 275973248 | bytes 7218343 | solution.py:196
  122.8 2.7 constant_dynamic-slice_fusion.8
  125.7 3.9 fusion.132
  129.6 1.0 reduce_sum.84
  130.6 1.0 multiply_reduce_fusion.2
  131.7 1.1 copy.85
  132.7 1.5 fusion.65
  134.3 1.8 multiply_convert_fusion.1
  136.8 1.6 pad_maximum_fusion.2
  139.3 11.6 %while.40 = (s32[]{:T(128)}, f32[128,8,64]{0,2,1:T(8,128)}, s32[]{:T(128)}, bf16[2048,512]{0,1:T(8,128)(2,1)}, bf16[2048,512]{0,1:T(8,128)(2,1)}, /*index=5*/bf1...) while((s32[]{:T(128)}, f32[128,8,64]{0,2,1:T(8,128)}, ...), condition=%wide.region_17.18_spmd.clone, body=%wide.region_16.17_spmd.clone.sunk | while | flops 415433856 | bytes 16786608 | solution.py:236
  139.3 2.7 constant_dynamic-slice_fusion.9
  142.0 2.8 fusion.138
  145.0 5.8 %fusion.139 = f32[128,8,64]{0,2,1:T(8,128)} fusion(f32[128,8,64]{0,2,1:T(8,128)} %get-tuple-element.860, bf16[1024,8,64]{0,2,1:T(8,128)(2,1)S(1)} %bitcast.180, f32[8,1024,128]{2,1,0:T(8,128)} %fusion.138, bf16[1024,8,64]{0,2,1:T(8,128)(2,1)} %bitcast.183, bf16[128,8,64]{0,2,1:T(8,128)(2,1)} %get-tuple-element.876, ...), kind=kOutput, calls=%fused_computation.62.clone.1 | convolution fusion | flops 281083904 | bytes 7077888 | tf_op jit(solution)/shard_map/while/body/hqk,khd->qhd/dot_general | solution.py:231
  150.8 1.8 copy.94
  152.6 2.1 convolution_convert_fusion.1
  154.7 41.7 %all-gather.5.cloned.1.call-done = bf16[2048,1024]{1,0:T(8,128)(2,1)} async-done(((bf16[128,1024]{1,0:T(8,128)(2,1)}), bf16[2048,1024]{1,0:T(8,128)(2,1)}) %all-gather.5.cloned.1.call-update) | async-done | bytes 4194320 | tf_op jit(solution)/shard_map/all_gather | solution.py:18
  196.4 4.5 %fusion.83 = (bf16[2048,512]{1,0:T(8,128)(2,1)}, bf16[2048,512]{1,0:T(8,128)(2,1)}) fusion(bf16[2048,1024]{1,0:T(8,128)(2,1)} %all-gather.5.cloned.1.call-done), kind=kLoop, calls=%fused_computation.160 | loop fusion | bytes 8388608 | tf_op jit(solution)/shard_map/split | solution.py:18
  200.9 4.0 copy.88
  204.9 4.0 copy.89
  209.6 39.0 %while.39 = (s32[]{:T(128)}, f32[128,8,64]{0,2,1:T(8,128)S(1)}, f32[128,8,64]{0,2,1:T(8,128)}, s32[]{:T(128)}, bf16[2048,512]{0,1:T(8,128)(2,1)}, /*index=5*/bf1...) while((s32[]{:T(128)}, f32[128,8,64]{0,2,1:T(8,128)S(1)}, ...), condition=%wide.region_15.16_spmd.clone, body=%wide.region_11.15_spmd.clone.sunk | while | flops 557058176 | bytes 24783208 | solution.py:276
  211.5 17.6 %conditional.3 = ((f32[128,8,64]{0,2,1:T(8,128)S(1)}, f32[128,8,64]{0,2,1:T(8,128)})) conditional(s32[]{:T(128)} %convert_element_type.220, (f32[128,8,64]{0,2,1:T(8,128)S(1)}, f32[128,8,64]{0,2,1:T(8,128)}) %tuple.126, (s32[]{:T(128)}, s32[1024]{0:T(1024)S(1)}, s32[]{:T(128)}, bf16[2048,512]{0,1:T(8,128)(2,1)}, bf16[128,8,64]{0,2,1:T(8,128)(2,1)}, ...), branch_computations={%region_13.13_spmd, %region_14.14_spmd} | conditional | flops 557056128 | bytes 24778362 | solution.py:272
  212.2 2.7 constant_dynamic-slice_fusion
  214.9 2.8 fusion.88
  218.6 5.9 %fusion.11 = f32[128,8,64]{0,2,1:T(8,128)} fusion(f32[128,8,64]{0,2,1:T(8,128)} %copy-done.8, bf16[1024,8,64]{0,2,1:T(8,128)(2,1)S(1)} %bitcast.182, f32[8,1024,128]{2,1,0:T(8,128)} %fusion.88, bf16[1024,8,64]{0,2,1:T(8,128)(2,1)} %bitcast.186, bf16[128,8,64]{0,2,1:T(8,128)(2,1)} %get-tuple-element.319, pred[1024,128]{1,0:T(8,128)(4,1)} %broadcast_compare_fusion), kind=kOutput, calls=%fused_computation.18 | convolution fusion | flops 281083904 | bytes 7077888 | tf_op jit(solution)/shard_map/while/body/eval_jaxpr/cond/branch_1_fun/hqk,qhd->khd/dot_general | solution.py:264
  224.4 4.7 %fusion.10 = f32[128,8,64]{0,2,1:T(8,128)} fusion(f32[128,8,64]{0,2,1:T(8,128)} %get-tuple-element.322, bf16[1024,8,64]{0,2,1:T(8,128)(2,1)} %bitcast.187, f32[8,1024,128]{2,1,0:T(8,128)} %fusion.88, pred[1024,128]{1,0:T(8,128)(4,1)} %broadcast_compare_fusion), kind=kOutput, calls=%fused_computation.17 | convolution fusion | flops 141623296 | bytes 5898240 | tf_op jit(solution)/shard_map/while/body/eval_jaxpr/cond/branch_1_fun/hqk,qhd->khd/dot_general | solution.py:267
  231.0 17.6 %conditional.3 = ((f32[128,8,64]{0,2,1:T(8,128)S(1)}, f32[128,8,64]{0,2,1:T(8,128)})) conditional(s32[]{:T(128)} %convert_element_type.220, (f32[128,8,64]{0,2,1:T(8,128)S(1)}, f32[128,8,64]{0,2,1:T(8,128)}) %tuple.126, (s32[]{:T(128)}, s32[1024]{0:T(1024)S(1)}, s32[]{:T(128)}, bf16[2048,512]{0,1:T(8,128)(2,1)}, bf16[128,8,64]{0,2,1:T(8,128)(2,1)}, ...), branch_computations={%region_13.13_spmd, %region_14.14_spmd} | conditional | flops 557056128 | bytes 24778362 | solution.py:272
  231.7 2.7 constant_dynamic-slice_fusion
  234.4 2.8 fusion.88
  238.1 5.9 %fusion.11 = f32[128,8,64]{0,2,1:T(8,128)} fusion(f32[128,8,64]{0,2,1:T(8,128)} %copy-done.8, bf16[1024,8,64]{0,2,1:T(8,128)(2,1)S(1)} %bitcast.182, f32[8,1024,128]{2,1,0:T(8,128)} %fusion.88, bf16[1024,8,64]{0,2,1:T(8,128)(2,1)} %bitcast.186, bf16[128,8,64]{0,2,1:T(8,128)(2,1)} %get-tuple-element.319, pred[1024,128]{1,0:T(8,128)(4,1)} %broadcast_compare_fusion), kind=kOutput, calls=%fused_computation.18 | convolution fusion | flops 281083904 | bytes 7077888 | tf_op jit(solution)/shard_map/while/body/eval_jaxpr/cond/branch_1_fun/hqk,qhd->khd/dot_general | solution.py:264
  243.9 4.7 %fusion.10 = f32[128,8,64]{0,2,1:T(8,128)} fusion(f32[128,8,64]{0,2,1:T(8,128)} %get-tuple-element.322, bf16[1024,8,64]{0,2,1:T(8,128)(2,1)} %bitcast.187, f32[8,1024,128]{2,1,0:T(8,128)} %fusion.88, pred[1024,128]{1,0:T(8,128)(4,1)} %broadcast_compare_fusion), kind=kOutput, calls=%fused_computation.17 | convolution fusion | flops 141623296 | bytes 5898240 | tf_op jit(solution)/shard_map/while/body/eval_jaxpr/cond/branch_1_fun/hqk,qhd->khd/dot_general | solution.py:267
  249.3 1.1 copy.93
  250.4 1.1 copy.95
  251.5 1.8 fusion.47
  253.3 2.1 convolution_convert_fusion
  256.6 2.0 convolution_convert_fusion.2
  259.5 1.8 scatter_custom_fusion.1
  262.2 1.2 convert_element_type.136
  263.4 1.2 fusion.85
  264.5 7.3 %all-to-all-start.2 = ((bf16[128,1,2,512]{3,2,1,0:T(2,128)(2,1)}), bf16[128,1,2,512]{3,2,1,0:T(2,128)(2,1)S(1)}, u32[]{:S(2)}, u32[]{:S(2)}) async-start(bf16[128,1,2,512]{3,2,1,0:T(2,128)(2,1)} %get-tuple-element.591), calls=%async_computation.2 | async-start | bytes 524288 | tf_op jit(solution)/shard_map/all_to_all | solution.py:44
  272.3 1.6 reduce.5
  274.0 9.4 %all-to-all-done.2 = bf16[128,1,2,512]{3,2,1,0:T(2,128)(2,1)S(1)} async-done(((bf16[128,1,2,512]{3,2,1,0:T(2,128)(2,1)}), bf16[128,1,2,512]{3,2,1,0:T(2,128)(2,1)S(1)}, u32[]{:S(2)}, u32[]{:S(2)}) %all-to-all-start.2) | async-done | bytes 262176 | tf_op jit(solution)/shard_map/all_to_all | solution.py:44
  283.5 5.3 %all-to-all-start.3 = ((bf16[128,1,2,512]{3,2,1,0:T(2,128)(2,1)}), bf16[128,1,2,512]{3,2,1,0:T(2,128)(2,1)}, u32[]{:S(2)}, u32[]{:S(2)}) async-start(bf16[128,1,2,512]{3,2,1,0:T(2,128)(2,1)} %get-tuple-element.592), calls=%async_computation.3 | async-start | bytes 524288 | tf_op jit(solution)/shard_map/all_to_all | solution.py:44
  288.8 1.9 fusion.45
  290.8 8.9 %all-to-all-done.3 = bf16[128,1,2,512]{3,2,1,0:T(2,128)(2,1)} async-done(((bf16[128,1,2,512]{3,2,1,0:T(2,128)(2,1)}), bf16[128,1,2,512]{3,2,1,0:T(2,128)(2,1)}, u32[]{:S(2)}, u32[]{:S(2)}) %all-to-all-start.3) | async-done | bytes 262176 | tf_op jit(solution)/shard_map/all_to_all | solution.py:44
  299.7 2.4 fusion.61
  302.1 1.3 reshape.449
  304.4 5.2 %scatter_custom_fusion.2 = f32[512,512]{1,0:T(8,128)} fusion(s32[512]{0:T(512)S(1)} %bitcast.200, f32[512,512]{1,0:T(8,128)} %reshape.449, f32[]{:T(128)} %constant.155.clone.1), kind=kCustom, calls=%fused_computation.89 | custom fusion | flops 262144 | bytes 1049088 | tf_op jit(solution)/shard_map/scatter-add | solution.py:323
  309.6 3.2 scatter_custom_fusion.3
  312.9 100.2 %all-reduce.5.cloned.1.call-done = (bf16[128,512]{1,0:T(8,128)(2,1)}, bf16[512,2048]{1,0:T(8,128)(2,1)}, bf16[512,512]{1,0:T(8,128)(2,1)}) async-done(((bf16[128,512]{1,0:T(8,128)(2,1)}, bf16[512,2048]{1,0:T(8,128)(2,1)}, bf16[512,512]{1,0:T(8,128)(2,1)}), (bf16[128,512]{1,0:T(8,128)(2,1)}, bf16[512,2048]{1,0:T(8,128)(2,1)}, bf16[512,512]{1,0:T(8,128)(2,1)})) %all-reduce.5.cloned.1.call-update) | async-done | bytes 2752528 | tf_op jit(solution)/shard_map/psum | solution.py:295
  413.0 4.2 convert_multiply_fusion
  417.3 1.1 convert_multiply_fusion.1
  (128 shorter events, 21.6 us)
Async XLA Ops:
  7.2 52.4 %copy-start = (bf16[512,2048]{1,0:T(8,128)(2,1)S(1)}, bf16[512,2048]{1,0:T(8,128)(2,1)}, u32[]{:S(2)}) copy-start(bf16[512,2048]{1,0:T(8,128)(2,1)} %param.21) | copy-start | bytes 6291460
  7.2 28.7 %copy-start.4 = (bf16[2048,128]{1,0:T(8,128)(2,1)S(1)}, bf16[2048,128]{1,0:T(8,128)(2,1)}, u32[]{:S(2)}) copy-start(bf16[2048,128]{1,0:T(8,128)(2,1)} %param.19) | copy-start | bytes 1572868
  8.9 35.4 %copy-start.26 = (s32[128]{0:T(128)}, s32[128]{0:T(128)S(1)}, u32[]{:S(2)}) copy-start(s32[128]{0:T(128)S(1)} %fusion.76) | copy-start | bytes 1540
  31.0 0.7 copy-start.13
  31.7 12.6 %copy-start.27 = (s32[128]{0:T(128)S(1)}, s32[128]{0:T(128)}, u32[]{:S(2)}) copy-start(s32[128]{0:T(128)} %param.17) | copy-start | bytes 1540
  34.8 23.7 %copy-start.15 = (bf16[128,512]{1,0:T(8,128)(2,1)S(1)}, bf16[128,512]{1,0:T(8,128)(2,1)}, u32[]{:S(2)}) copy-start(bf16[128,512]{1,0:T(8,128)(2,1)} %param.20) | copy-start | bytes 393220
  39.7 17.9 %all-to-all-start.1 = ((bf16[128,4,512]{2,1,0:T(4,128)(2,1)}), bf16[128,4,512]{2,1,0:T(4,128)(2,1)S(1)}, u32[]{:S(2)}, u32[]{:S(2)}) async-start(bf16[128,4,512]{2,1,0:T(4,128)(2,1)} %pad_select_fusion), calls=%async_computation.1 | async-start | bytes 1048576 | tf_op jit(solution)/shard_map/all_to_all | solution.py:142
  44.2 65.4 %all-gather.3.cloned.1.call-start = ((), (), s32[]{:S(2)}) async-start(), calls=%async_computation.4 | async-start | bytes 4456448 | tf_op jit(solution)/shard_map/all_gather | solution.py:18
  44.9 16.2 %copy-start.23 = (pred[128]{0:T(512)(128)(4,1)}, pred[128]{0:T(512)(128)(4,1)S(1)}, u32[]{:S(2)}) copy-start(pred[128]{0:T(512)(128)(4,1)S(1)} %get-tuple-element.603) | copy-start | bytes 388
  58.6 0.7 copy-start.17
  58.8 0.7 copy-start.1
  58.8 2.2 copy-start.19
  59.5 1.5 copy-start.21
  61.0 53.1 %copy-start.12 = (bf16[128,2048]{1,0:T(8,128)(2,1)}, bf16[128,2048]{1,0:T(8,128)(2,1)S(1)}, u32[]{:S(2)}) copy-start(bf16[128,2048]{1,0:T(8,128)(2,1)S(1)} %get-tuple-element.606) | copy-start | bytes 1572868
  61.1 53.1 %copy-start.6 = (bf16[128,512]{1,0:T(8,128)(2,1)}, bf16[128,512]{1,0:T(8,128)(2,1)S(1)}, u32[]{:S(2)}) copy-start(bf16[128,512]{1,0:T(8,128)(2,1)S(1)} %get-tuple-element.593) | copy-start | bytes 393220
  62.0 134.4 %all-gather.5.cloned.1.call-start = ((), (), s32[]{:S(2)}) async-start(), calls=%async_computation.5 | async-start | bytes 4456448 | tf_op jit(solution)/shard_map/all_gather | solution.py:18
  138.5 274.5 %all-reduce.5.cloned.1.call-start = ((), (), s32[]{:S(2)}) async-start(), calls=%async_computation.6 | async-start | bytes 5505024 | tf_op jit(solution)/shard_map/psum | solution.py:295
  209.6 43.7 %copy-start.2 = (f32[128,512]{1,0:T(8,128)S(1)}, f32[128,512]{1,0:T(8,128)}, u32[]{:S(2)}) copy-start(f32[128,512]{1,0:T(8,128)} %copy-done.1) | copy-start | bytes 786436
  209.6 43.7 %copy-start.20 = (f32[128]{0:T(128)S(1)}, f32[128]{0:T(128)}, u32[]{:S(2)}) copy-start(f32[128]{0:T(128)} %copy-done.19) | copy-start | bytes 1540
  209.6 43.7 %copy-start.22 = (f32[128]{0:T(128)S(1)}, f32[128]{0:T(128)}, u32[]{:S(2)}) copy-start(f32[128]{0:T(128)} %copy-done.21) | copy-start | bytes 1540
  211.5 0.7 copy-start.8
  224.4 4.7 %copy-start.9 = (f32[128,8,64]{0,2,1:T(8,128)S(1)}, f32[128,8,64]{0,2,1:T(8,128)}, u32[]{:S(2)}) copy-start(f32[128,8,64]{0,2,1:T(8,128)} %fusion.11) | copy-start | bytes 786436 | tf_op jit(solution)/shard_map/while/body/eval_jaxpr/cond
  231.0 0.7 copy-start.8
  243.9 4.7 %copy-start.9 = (f32[128,8,64]{0,2,1:T(8,128)S(1)}, f32[128,8,64]{0,2,1:T(8,128)}, u32[]{:S(2)}) copy-start(f32[128,8,64]{0,2,1:T(8,128)} %fusion.11) | copy-start | bytes 786436 | tf_op jit(solution)/shard_map/while/body/eval_jaxpr/cond
  248.6 0.7 copy-start.10
  251.5 4.9 %copy-start.5 = (bf16[128,512]{1,0:T(8,128)(2,1)S(1)}, bf16[128,512]{1,0:T(8,128)(2,1)}, u32[]{:S(2)}) copy-start(bf16[128,512]{1,0:T(8,128)(2,1)} %param.23) | copy-start | bytes 393220
  251.5 5.1 %copy-start.25 = (pred[128]{0:T(512)(128)(4,1)S(1)}, pred[128]{0:T(512)(128)(4,1)}, u32[]{:S(2)}) copy-start(pred[128]{0:T(512)(128)(4,1)} %get-tuple-element.602) | copy-start | bytes 388
  255.5 3.1 copy-start.16
  255.5 4.0 copy-start.24
  256.6 2.0 copy-start.3
  258.5 30.3 %copy-start.7 = (bf16[128,512]{1,0:T(8,128)(2,1)S(1)}, bf16[128,512]{1,0:T(8,128)(2,1)}, u32[]{:S(2)}) copy-start(bf16[128,512]{1,0:T(8,128)(2,1)} %get-tuple-element.587) | copy-start | bytes 393220
  264.5 19.0 %all-to-all-start.2 = ((bf16[128,1,2,512]{3,2,1,0:T(2,128)(2,1)}), bf16[128,1,2,512]{3,2,1,0:T(2,128)(2,1)S(1)}, u32[]{:S(2)}, u32[]{:S(2)}) async-start(bf16[128,1,2,512]{3,2,1,0:T(2,128)(2,1)} %get-tuple-element.591), calls=%async_computation.2 | async-start | bytes 524288 | tf_op jit(solution)/shard_map/all_to_all | solution.py:44
  283.5 7.3 %copy-start.11 = (bf16[128,1,2,512]{3,2,1,0:T(2,128)(2,1)}, bf16[128,1,2,512]{3,2,1,0:T(2,128)(2,1)S(1)}, u32[]{:S(2)}) copy-start(bf16[128,1,2,512]{3,2,1,0:T(2,128)(2,1)S(1)} %all-to-all-done.2) | copy-start | bytes 786436
  283.5 16.2 %all-to-all-start.3 = ((bf16[128,1,2,512]{3,2,1,0:T(2,128)(2,1)}), bf16[128,1,2,512]{3,2,1,0:T(2,128)(2,1)}, u32[]{:S(2)}, u32[]{:S(2)}) async-start(bf16[128,1,2,512]{3,2,1,0:T(2,128)(2,1)} %get-tuple-element.592), calls=%async_computation.3 | async-start | bytes 524288 | tf_op jit(solution)/shard_map/all_to_all | solution.py:44
  413.0 4.2 copy-start.14
  413.0 5.3 %copy-start.18 = (bf16[128,512]{1,0:T(8,128)(2,1)S(1)}, bf16[128,512]{1,0:T(8,128)(2,1)}, u32[]{:S(2)}) copy-start(bf16[128,512]{1,0:T(8,128)(2,1)} %get-tuple-element.571) | copy-start | bytes 393220
Sparse Core Ops, SparseCore 0:
  62.1 47.4 all-gather.2
  138.6 57.7 all-gather.4
  258.7 154.2 all-reduce.4
where the time goes:
time: 427 us; the launch traced here: 426 us
  waiting for transfers between devices  219 us (51%)
  local copies, waits for them, and re-layouts  60.9 us (14%)
  matrix products  53.4 us (13%)
  other arithmetic  37.6 us (9%)
  blocking collectives  20.9 us (5%)
  starting transfers between devices  17.2 us (4%)
  between operations  14.2 us (3%)
    psum x1, waiting for transfers between devices, local(): lax.psum(projection_local.astype(jnp.bfloat16), ('dp', 'cp'))  100 us
    all_gather x2, waiting for transfers between devices, side_by_side(): lax.all_gather(both, axis, axis=dim, tiled=True)  87.6 us
    all_to_all x1, blocking collectives, local(): lax.all_to_all(requests, ('dp', 'cp'), split_axis=0, concat_axis=0, tiled...  20.9 us
    all_to_all x2, waiting for transfers between devices, several_exchanges(): lax.all_to_all(piece, axis, split_axis=0, concat_axis=0, tiled=True)  18.4 us
    unnamed x56, local copies, waits for them, and re-layouts  17.1 us
    all_to_all x1, waiting for transfers between devices, local(): lax.all_to_all(packed, ('dp', 'cp'), split_axis=0, concat_axis=0, tiled=T...  12.7 us
    all_to_all x2, starting transfers between devices, several_exchanges(): lax.all_to_all(piece, axis, split_axis=0, concat_axis=0, tiled=True)  12.6 us
    dot_general x2, matrix products, accumulate(): jnp.einsum('hqk,qhd->khd', delta_scores, query_block, preferred_element_t...  11.7 us
  transfers between devices with their start and end apart: 6, of which 6 were waited for; matrix products, arithmetic and copies ran while one was open for 10% of the time, Pallas kernels for 0%

commit v1 on v0

--- a/solution.py
+++ b/solution.py
@@ -292,7 +292,7 @@
     joined_sum, output_sum, projection_sum = (
         lax.psum(joined_local.astype(jnp.bfloat16), ("dp", "cp")).astype(jnp.float32),
         lax.psum(output_local.astype(jnp.bfloat16), ("dp", "cp")).astype(jnp.float32),
-        lax.psum(projection_local.astype(jnp.bfloat16), ("dp", "cp")).astype(jnp.float32),
+        lax.psum(lax.psum(projection_local.astype(jnp.bfloat16), "cp"), "dp").astype(jnp.float32),
     )
     norm_scale = (tokens_here * devices) ** (-0.5)
     cold_event = jnp.where(

time: 427 us -> 571 us (1.34)
  waiting for transfers between devices: 219 us -> 361 us
    psum x1 -> x3, waiting for transfers between devices: 100 us -> 250 us  [the longest x1 144 us: local(): lax.psum(joined_local.astype(jnp.bfloat16), ('dp', 'cp'))]
    all_to_all x2, waiting for transfers between devices: 18.4 us -> 8.85 us  [several_exchanges(): lax.all_to_all(piece, axis, split_axis=0, concat_axis=0, tiled=True)]
    unnamed x56 -> x52, local copies, waits for them, and re-layouts: 17.1 us -> 16.4 us
  transfers between devices with their start and end apart: 6 -> 8, of which waited for: 6 -> 7; matrix products, arithmetic and copies ran while one was open for 10% -> 8% of each run, Pallas kernels for 0% -> 0%
where the time goes in v1:
time: 571 us; the launch traced here: 570 us
  waiting for transfers between devices  361 us (63%)
  local copies, waits for them, and re-layouts  60 us (11%)
  matrix products  52.6 us (9%)
  other arithmetic  38.4 us (7%)
  blocking collectives  20.9 us (4%)
  starting transfers between devices  19.7 us (3%)
  between operations  14.3 us (3%)
    psum x1, waiting for transfers between devices, local(): lax.psum(joined_local.astype(jnp.bfloat16), ('dp', 'cp'))  144 us
    all_gather x2, waiting for transfers between devices, side_by_side(): lax.all_gather(both, axis, axis=dim, tiled=True)  89.7 us
    psum x1, waiting for transfers between devices, local(): lax.psum(projection_local.astype(jnp.bfloat16), 'cp')  78.9 us
    psum x1, waiting for transfers between devices, local(): lax.psum(lax.psum(projection_local.astype(jnp.bfloat16), 'cp'), 'dp')  26.5 us
    all_to_all x1, blocking collectives, local(): lax.all_to_all(requests, ('dp', 'cp'), split_axis=0, concat_axis=0, tiled...  20.9 us
    unnamed x52, local copies, waits for them, and re-layouts  16.4 us
    all_to_all x2, starting transfers between devices, several_exchanges(): lax.all_to_all(piece, axis, split_axis=0, concat_axis=0, tiled=True)  14.8 us
    all_to_all x1, waiting for transfers between devices, local(): lax.all_to_all(packed, ('dp', 'cp'), split_axis=0, concat_axis=0, tiled=T...  12.8 us
  transfers between devices with their start and end apart: 8, of which 7 were waited for; matrix products, arithmetic and copies ran while one was open for 8% of the time, Pallas kernels for 0%

profile of v1, /device:TPU:1, one launch (start us, length us, event | category | flops | bytes accessed | tf_op | source)
XLA Modules:
  0.0 569.5 jit_solution(1757749743465349953)
XLA Ops:
  8.9 1.1 scatter_custom_fusion
  10.1 20.9 %all_to_all.27 = s32[128,1,4]{2,1,0:T(1,128)S(1)} all-to-all(s32[128,1,4]{2,1,0:T(1,128)S(1)} %bitcast.196), channel_id=1, replica_groups=mesh['dp'=8,'cp'=16] {'dp','cp'}, dimensions={0} | all-to-all | bytes 4096 | tf_op jit(solution)/shard_map/all_to_all | solution.py:128
  31.7 3.1 gather_fusion
  35.9 1.3 gather_fusion.1
  37.5 2.2 pad_select_fusion
  39.7 4.5 all-to-all-start.1
  44.8 12.8 %all-to-all-done.1 = bf16[128,4,512]{2,1,0:T(4,128)(2,1)S(1)} async-done(((bf16[128,4,512]{2,1,0:T(4,128)(2,1)}), bf16[128,4,512]{2,1,0:T(4,128)(2,1)S(1)}, u32[]{:S(2)}, u32[]{:S(2)}) %all-to-all-start.1) | async-done | bytes 524320 | tf_op jit(solution)/shard_map/all_to_all | solution.py:142
  59.5 1.5 multiply_convert_fusion
  63.7 45.9 %all-gather.3.cloned.1.call-done = bf16[2048,1024]{1,0:T(8,128)(2,1)} async-done(((bf16[128,1024]{1,0:T(8,128)(2,1)}), bf16[2048,1024]{1,0:T(8,128)(2,1)}) %all-gather.3.cloned.1.call-update) | async-done | bytes 4194320 | tf_op jit(solution)/shard_map/all_gather | solution.py:18
  109.6 4.5 fusion.84
  114.1 4.0 copy.83
  118.1 4.0 copy.84
  122.7 6.8 %while.38 = (s32[]{:T(128)}, f32[128,8,64]{0,2,1:T(8,128)}, s32[]{:T(128)}, bf16[2048,512]{0,1:T(8,128)(2,1)}, bf16[2048,512]{0,1:T(8,128)(2,1)}, /*index=5*/bf1...) while((s32[]{:T(128)}, f32[128,8,64]{0,2,1:T(8,128)}, ...), condition=%wide.region_5.6_spmd.clone, body=%wide.region_4.5_spmd.clone.sunk | while | flops 275973248 | bytes 7218343 | solution.py:196
  122.7 2.7 constant_dynamic-slice_fusion.8
  125.6 3.9 fusion.132
  129.5 1.0 reduce_sum.84
  130.6 1.0 multiply_reduce_fusion.2
  131.6 1.1 copy.85
  132.7 1.5 fusion.65
  134.2 1.8 multiply_convert_fusion.1
  136.8 1.6 pad_maximum_fusion.2
  139.2 11.6 %while.40 = (s32[]{:T(128)}, f32[128,8,64]{0,2,1:T(8,128)}, s32[]{:T(128)}, bf16[2048,512]{0,1:T(8,128)(2,1)}, bf16[2048,512]{0,1:T(8,128)(2,1)}, /*index=5*/bf1...) while((s32[]{:T(128)}, f32[128,8,64]{0,2,1:T(8,128)}, ...), condition=%wide.region_17.18_spmd.clone, body=%wide.region_16.17_spmd.clone.sunk | while | flops 415433856 | bytes 16786608 | solution.py:236
  139.2 2.7 constant_dynamic-slice_fusion.9
  141.9 2.8 fusion.138
  145.0 5.8 %fusion.139 = f32[128,8,64]{0,2,1:T(8,128)} fusion(f32[128,8,64]{0,2,1:T(8,128)} %get-tuple-element.859, bf16[1024,8,64]{0,2,1:T(8,128)(2,1)S(1)} %bitcast.180, f32[8,1024,128]{2,1,0:T(8,128)} %fusion.138, bf16[1024,8,64]{0,2,1:T(8,128)(2,1)} %bitcast.183, bf16[128,8,64]{0,2,1:T(8,128)(2,1)} %get-tuple-element.875, ...), kind=kOutput, calls=%fused_computation.62.clone.1 | convolution fusion | flops 281083904 | bytes 7077888 | tf_op jit(solution)/shard_map/while/body/hqk,khd->qhd/dot_general | solution.py:231
  150.8 1.8 copy.94
  152.6 43.8 %all-gather.5.cloned.1.call-done = bf16[2048,1024]{1,0:T(8,128)(2,1)} async-done(((bf16[128,1024]{1,0:T(8,128)(2,1)}), bf16[2048,1024]{1,0:T(8,128)(2,1)}) %all-gather.5.cloned.1.call-update) | async-done | bytes 4194320 | tf_op jit(solution)/shard_map/all_gather | solution.py:18
  196.4 4.5 fusion.83
  200.9 4.0 copy.88
  204.9 4.0 copy.89
  209.6 39.1 %while.39 = (s32[]{:T(128)}, f32[128,8,64]{0,2,1:T(8,128)S(1)}, f32[128,8,64]{0,2,1:T(8,128)}, s32[]{:T(128)}, bf16[2048,512]{0,1:T(8,128)(2,1)}, /*index=5*/bf1...) while((s32[]{:T(128)}, f32[128,8,64]{0,2,1:T(8,128)S(1)}, ...), condition=%wide.region_15.16_spmd.clone, body=%wide.region_11.15_spmd.clone.sunk | while | flops 557058176 | bytes 24783208 | solution.py:276
  211.5 17.7 %conditional.3 = ((f32[128,8,64]{0,2,1:T(8,128)S(1)}, f32[128,8,64]{0,2,1:T(8,128)})) conditional(s32[]{:T(128)} %convert_element_type.220, (f32[128,8,64]{0,2,1:T(8,128)S(1)}, f32[128,8,64]{0,2,1:T(8,128)}) %tuple.126, (s32[]{:T(128)}, s32[1024]{0:T(1024)S(1)}, s32[]{:T(128)}, bf16[2048,512]{0,1:T(8,128)(2,1)}, bf16[128,8,64]{0,2,1:T(8,128)(2,1)}, ...), branch_computations={%region_13.13_spmd, %region_14.14_spmd} | conditional | flops 557056128 | bytes 24778362 | solution.py:272
  212.2 2.7 constant_dynamic-slice_fusion
  214.9 2.8 fusion.88
  218.6 5.9 %fusion.11 = f32[128,8,64]{0,2,1:T(8,128)} fusion(f32[128,8,64]{0,2,1:T(8,128)} %copy-done.8, bf16[1024,8,64]{0,2,1:T(8,128)(2,1)S(1)} %bitcast.182, f32[8,1024,128]{2,1,0:T(8,128)} %fusion.88, bf16[1024,8,64]{0,2,1:T(8,128)(2,1)} %bitcast.186, bf16[128,8,64]{0,2,1:T(8,128)(2,1)} %get-tuple-element.319, pred[1024,128]{1,0:T(8,128)(4,1)} %broadcast_compare_fusion), kind=kOutput, calls=%fused_computation.18 | convolution fusion | flops 281083904 | bytes 7077888 | tf_op jit(solution)/shard_map/while/body/eval_jaxpr/cond/branch_1_fun/hqk,qhd->khd/dot_general | solution.py:264
  224.5 4.7 fusion.10
  231.1 17.7 %conditional.3 = ((f32[128,8,64]{0,2,1:T(8,128)S(1)}, f32[128,8,64]{0,2,1:T(8,128)})) conditional(s32[]{:T(128)} %convert_element_type.220, (f32[128,8,64]{0,2,1:T(8,128)S(1)}, f32[128,8,64]{0,2,1:T(8,128)}) %tuple.126, (s32[]{:T(128)}, s32[1024]{0:T(1024)S(1)}, s32[]{:T(128)}, bf16[2048,512]{0,1:T(8,128)(2,1)}, bf16[128,8,64]{0,2,1:T(8,128)(2,1)}, ...), branch_computations={%region_13.13_spmd, %region_14.14_spmd} | conditional | flops 557056128 | bytes 24778362 | solution.py:272
  231.8 2.7 constant_dynamic-slice_fusion
  234.5 2.8 fusion.88
  238.2 5.9 %fusion.11 = f32[128,8,64]{0,2,1:T(8,128)} fusion(f32[128,8,64]{0,2,1:T(8,128)} %copy-done.8, bf16[1024,8,64]{0,2,1:T(8,128)(2,1)S(1)} %bitcast.182, f32[8,1024,128]{2,1,0:T(8,128)} %fusion.88, bf16[1024,8,64]{0,2,1:T(8,128)(2,1)} %bitcast.186, bf16[128,8,64]{0,2,1:T(8,128)(2,1)} %get-tuple-element.319, pred[1024,128]{1,0:T(8,128)(4,1)} %broadcast_compare_fusion), kind=kOutput, calls=%fused_computation.18 | convolution fusion | flops 281083904 | bytes 7077888 | tf_op jit(solution)/shard_map/while/body/eval_jaxpr/cond/branch_1_fun/hqk,qhd->khd/dot_general | solution.py:264
  244.1 4.7 fusion.10
  248.8 1.1 copy.93
  250.7 1.8 fusion.47
  253.8 2.0 convolution_convert_fusion.2
  255.8 1.1 convolution_convert_fusion.1
  256.9 78.9 %all-reduce.7.cloned.1.call-done = bf16[128,512]{1,0:T(8,128)(2,1)} async-done(((bf16[128,512]{1,0:T(8,128)(2,1)}), bf16[128,512]{1,0:T(8,128)(2,1)}) %all-reduce.7.cloned.1.call-update) | async-done | bytes 131088 | tf_op jit(solution)/shard_map/psum | solution.py:295
  336.1 2.1 convolution_convert_fusion
  339.2 1.8 scatter_custom_fusion.1
  341.9 1.2 convert_element_type.136
  343.0 1.2 fusion.85
  344.2 9.6 %all-to-all-start.2 = ((bf16[128,1,2,512]{3,2,1,0:T(2,128)(2,1)}), bf16[128,1,2,512]{3,2,1,0:T(2,128)(2,1)S(1)}, u32[]{:S(2)}, u32[]{:S(2)}) async-start(bf16[128,1,2,512]{3,2,1,0:T(2,128)(2,1)} %get-tuple-element.590), calls=%async_computation.2 | async-start | bytes 524288 | tf_op jit(solution)/shard_map/all_to_all | solution.py:44
  354.3 1.6 reduce.5
  356.0 8.8 %all-to-all-done.2 = bf16[128,1,2,512]{3,2,1,0:T(2,128)(2,1)S(1)} async-done(((bf16[128,1,2,512]{3,2,1,0:T(2,128)(2,1)}), bf16[128,1,2,512]{3,2,1,0:T(2,128)(2,1)S(1)}, u32[]{:S(2)}, u32[]{:S(2)}) %all-to-all-start.2) | async-done | bytes 262176 | tf_op jit(solution)/shard_map/all_to_all | solution.py:44
  364.9 5.2 all-to-all-start.3
  370.1 1.9 fusion.45
  372.1 26.5 %all-reduce.9.cloned.1.call-done = bf16[128,512]{1,0:T(8,128)(2,1)} async-done(((bf16[128,512]{1,0:T(8,128)(2,1)}), bf16[128,512]{1,0:T(8,128)(2,1)}) %all-reduce.9.cloned.1.call-update) | async-done | bytes 131088 | tf_op jit(solution)/shard_map/psum | solution.py:295
  398.6 1.6 convert_multiply_fusion.4
  400.2 2.4 fusion.61
  402.6 1.3 reshape.449
  404.9 5.2 scatter_custom_fusion.2
  410.1 3.2 scatter_custom_fusion.3
  413.4 144.3 %all-reduce.11.cloned.1.call-done = (bf16[512,2048]{1,0:T(8,128)(2,1)}, bf16[512,512]{1,0:T(8,128)(2,1)}) async-done(((bf16[512,2048]{1,0:T(8,128)(2,1)}, bf16[512,512]{1,0:T(8,128)(2,1)}), (bf16[512,2048]{1,0:T(8,128)(2,1)}, bf16[512,512]{1,0:T(8,128)(2,1)})) %all-reduce.11.cloned.1.call-update) | async-done | bytes 2621456 | tf_op jit(solution)/shard_map/psum | solution.py:293
  557.7 4.2 convert_multiply_fusion
  561.9 1.1 convert_multiply_fusion.1
  (130 shorter events, 22.3 us)
Async XLA Ops:
  7.2 52.4 %copy-start = (bf16[512,2048]{1,0:T(8,128)(2,1)S(1)}, bf16[512,2048]{1,0:T(8,128)(2,1)}, u32[]{:S(2)}) copy-start(bf16[512,2048]{1,0:T(8,128)(2,1)} %param.21) | copy-start | bytes 6291460
  7.2 28.7 %copy-start.4 = (bf16[2048,128]{1,0:T(8,128)(2,1)S(1)}, bf16[2048,128]{1,0:T(8,128)(2,1)}, u32[]{:S(2)}) copy-start(bf16[2048,128]{1,0:T(8,128)(2,1)} %param.19) | copy-start | bytes 1572868
  8.9 35.4 %copy-start.24 = (s32[128]{0:T(128)}, s32[128]{0:T(128)S(1)}, u32[]{:S(2)}) copy-start(s32[128]{0:T(128)S(1)} %fusion.76) | copy-start | bytes 1540
  31.0 0.7 copy-start.12
  31.7 12.6 %copy-start.25 = (s32[128]{0:T(128)S(1)}, s32[128]{0:T(128)}, u32[]{:S(2)}) copy-start(s32[128]{0:T(128)} %param.17) | copy-start | bytes 1540
  34.8 23.7 %copy-start.14 = (bf16[128,512]{1,0:T(8,128)(2,1)S(1)}, bf16[128,512]{1,0:T(8,128)(2,1)}, u32[]{:S(2)}) copy-start(bf16[128,512]{1,0:T(8,128)(2,1)} %param.20) | copy-start | bytes 393220
  39.7 17.9 %all-to-all-start.1 = ((bf16[128,4,512]{2,1,0:T(4,128)(2,1)}), bf16[128,4,512]{2,1,0:T(4,128)(2,1)S(1)}, u32[]{:S(2)}, u32[]{:S(2)}) async-start(bf16[128,4,512]{2,1,0:T(4,128)(2,1)} %pad_select_fusion), calls=%async_computation.1 | async-start | bytes 1048576 | tf_op jit(solution)/shard_map/all_to_all | solution.py:142
  44.2 65.4 %all-gather.3.cloned.1.call-start = ((), (), s32[]{:S(2)}) async-start(), calls=%async_computation.4 | async-start | bytes 4456448 | tf_op jit(solution)/shard_map/all_gather | solution.py:18
  44.8 16.3 %copy-start.21 = (pred[128]{0:T(512)(128)(4,1)}, pred[128]{0:T(512)(128)(4,1)S(1)}, u32[]{:S(2)}) copy-start(pred[128]{0:T(512)(128)(4,1)S(1)} %get-tuple-element.602) | copy-start | bytes 388
  58.6 0.7 copy-start.16
  58.8 0.7 copy-start.1
  58.8 2.2 copy-start.17
  59.5 1.5 copy-start.19
  61.0 53.1 %copy-start.11 = (bf16[128,2048]{1,0:T(8,128)(2,1)}, bf16[128,2048]{1,0:T(8,128)(2,1)S(1)}, u32[]{:S(2)}) copy-start(bf16[128,2048]{1,0:T(8,128)(2,1)S(1)} %get-tuple-element.605) | copy-start | bytes 1572868
  61.1 53.0 %copy-start.6 = (bf16[128,512]{1,0:T(8,128)(2,1)}, bf16[128,512]{1,0:T(8,128)(2,1)S(1)}, u32[]{:S(2)}) copy-start(bf16[128,512]{1,0:T(8,128)(2,1)S(1)} %get-tuple-element.592) | copy-start | bytes 393220
  61.9 134.4 %all-gather.5.cloned.1.call-start = ((), (), s32[]{:S(2)}) async-start(), calls=%async_computation.5 | async-start | bytes 4456448 | tf_op jit(solution)/shard_map/all_gather | solution.py:18
  138.5 197.3 %all-reduce.7.cloned.1.call-start = ((), (), s32[]{:S(2)}) async-start(), calls=%async_computation.6 | async-start | bytes 262144 | tf_op jit(solution)/shard_map/psum | solution.py:295
  209.6 43.0 %copy-start.2 = (f32[128,512]{1,0:T(8,128)S(1)}, f32[128,512]{1,0:T(8,128)}, u32[]{:S(2)}) copy-start(f32[128,512]{1,0:T(8,128)} %copy-done.1) | copy-start | bytes 786436
  209.6 43.0 %copy-start.18 = (f32[128]{0:T(128)S(1)}, f32[128]{0:T(128)}, u32[]{:S(2)}) copy-start(f32[128]{0:T(128)} %copy-done.17) | copy-start | bytes 1540
  209.6 43.0 %copy-start.20 = (f32[128]{0:T(128)S(1)}, f32[128]{0:T(128)}, u32[]{:S(2)}) copy-start(f32[128]{0:T(128)} %copy-done.19) | copy-start | bytes 1540
  211.5 0.7 copy-start.8
  224.5 4.7 copy-start.9
  231.1 0.7 copy-start.8
  244.1 4.7 copy-start.9
  248.7 4.8 copy-start.5
  248.7 5.0 copy-start.23
  248.8 7.0 %copy-start.7 = (bf16[128,512]{1,0:T(8,128)(2,1)S(1)}, bf16[128,512]{1,0:T(8,128)(2,1)}, u32[]{:S(2)}) copy-start(bf16[128,512]{1,0:T(8,128)(2,1)} %get-tuple-element.586) | copy-start | bytes 393220
  253.5 84.7 %copy-start.15 = (bf16[128,512]{1,0:T(8,128)(2,1)S(1)}, bf16[128,512]{1,0:T(8,128)(2,1)}, u32[]{:S(2)}) copy-start(bf16[128,512]{1,0:T(8,128)(2,1)} %param.20) | copy-start | bytes 393220
  253.5 85.6 %copy-start.22 = (pred[128]{0:T(512)(128)(4,1)S(1)}, pred[128]{0:T(512)(128)(4,1)}, u32[]{:S(2)}) copy-start(pred[128]{0:T(512)(128)(4,1)} %copy-done.21) | copy-start | bytes 388
  253.7 84.5 %copy-start.3 = (f32[128,512]{1,0:T(8,128)}, f32[128,512]{1,0:T(8,128)S(1)}, u32[]{:S(2)}) copy-start(f32[128,512]{1,0:T(8,128)S(1)} %convert_add_fusion) | copy-start | bytes 786436
  255.7 142.8 %all-reduce.9.cloned.1.call-start = ((), (), s32[]{:S(2)}) async-start(), calls=%async_computation.7 | async-start | bytes 262144 | tf_op jit(solution)/shard_map/psum | solution.py:295
  335.8 221.8 %all-reduce.11.cloned.1.call-start = ((), (), s32[]{:S(2)}) async-start(), calls=%async_computation.8 | async-start | bytes 5242880 | tf_op jit(solution)/shard_map/psum | solution.py:293
  344.2 20.7 %all-to-all-start.2 = ((bf16[128,1,2,512]{3,2,1,0:T(2,128)(2,1)}), bf16[128,1,2,512]{3,2,1,0:T(2,128)(2,1)S(1)}, u32[]{:S(2)}, u32[]{:S(2)}) async-start(bf16[128,1,2,512]{3,2,1,0:T(2,128)(2,1)} %get-tuple-element.590), calls=%async_computation.2 | async-start | bytes 524288 | tf_op jit(solution)/shard_map/all_to_all | solution.py:44
  364.9 35.3 %copy-start.10 = (bf16[128,1,2,512]{3,2,1,0:T(2,128)(2,1)}, bf16[128,1,2,512]{3,2,1,0:T(2,128)(2,1)S(1)}, u32[]{:S(2)}) copy-start(bf16[128,1,2,512]{3,2,1,0:T(2,128)(2,1)S(1)} %all-to-all-done.2) | copy-start | bytes 786436
  364.9 35.3 %all-to-all-start.3 = ((bf16[128,1,2,512]{3,2,1,0:T(2,128)(2,1)}), bf16[128,1,2,512]{3,2,1,0:T(2,128)(2,1)}, u32[]{:S(2)}, u32[]{:S(2)}) async-start(bf16[128,1,2,512]{3,2,1,0:T(2,128)(2,1)} %get-tuple-element.591), calls=%async_computation.3 | async-start | bytes 524288 | tf_op jit(solution)/shard_map/all_to_all | solution.py:44
  557.7 4.2 copy-start.13
Sparse Core Ops, SparseCore 0:
  62.1 47.4 all-gather.2
  138.6 57.7 all-gather.4
  255.9 79.8 all-reduce.6
  338.0 60.5 all-reduce.8
  404.0 153.6 all-reduce.10
